TPU v7x, 32 devices: a whole 2x2x4 slice. The times are simulated.
32 devices in a mesh: parts: 2 (over y), fsdp: 8 (over z, x), rep: 2 (over core).
Axes of the slice: x: 2, y: 2, z: 4, core: 2. Of those that a mesh axis runs over, the one named last changes fastest.
Arguments:
- tokens: bfloat16 [2, 4096, 5120], P('rep', ('parts', 'fsdp')), parts along dimension 1, may hold values from -6 to 6
- cotangent: bfloat16 [2, 4096, 8], P('rep', ('parts', 'fsdp')), parts along dimension 1, may hold values from -0.1875 to 0.1875
- params: float32 [16, 5120], P(('parts', 'fsdp')), parts along dimension 0, may hold values from -0.078125 to 0.078125
- momentum: float32 [2, 16, 5120], P('rep', ('parts', 'fsdp')), parts along dimension 1, may hold values from -6 to 6
- indices: int32 [2, 16, 40, 16], P('rep', ('parts', 'fsdp')), parts along dimension 1, may hold values from 0 to 127, all different within a row
Outputs:
- new_params: float32 [16, 5120], P(('parts', 'fsdp')), parts along dimension 0
- new_momentum: float32 [2, 16, 5120], P('rep', ('parts', 'fsdp')), parts along dimension 1
There are 2 independent parts, one for each index of `parts`. A program takes and returns all parts, laid end to end along the dimension named above; each array names one. Nothing has to cross between parts.
Inputs may be any that keep to these rules, and one draw needn't show every extreme that they name: Within each block the 16 indices are distinct.
All inputs are finite; a program needn't handle non-finite values.
Results may differ from a plain program's by a relative error of at most 0.0003.
Values sent between devices are 32-bit elements; how exact they have to be, the bound alone decides.
A program may use at most 64 MiB of HBM per device.

v0:
```python
import jax
import jax.numpy as jnp
from jax import lax
from jax.sharding import PartitionSpec as P

SPAN = 128


momentum_decay = 0.9
learn_rate = 0.5


def span_basis(length):
    freq = jnp.arange(length, dtype=jnp.float32)[:, None]
    place = jnp.arange(length, dtype=jnp.float32)[None, :]
    scale = jnp.where(freq == 0.0, jnp.sqrt(1.0 / length), jnp.sqrt(2.0 / length))
    return scale * jnp.cos(jnp.pi * (2.0 * place + 1.0) * freq / (2.0 * length))


def local(tokens, cotangent, params, momentum, indices):
    local_tokens = tokens[0]
    local_cot = cotangent[0]
    width = local_tokens.shape[1]
    blocks_row = width // SPAN
    high = lax.Precision.HIGHEST
    basis = span_basis(SPAN)
    slots = jnp.arange(SPAN, dtype=jnp.int32)
    picks = indices[0]
    selector = (picks[..., None] == slots).astype(jnp.float32)
    gradient = lax.psum_scatter(
        lax.dot_general(
            local_cot, local_tokens, (((0,), (0,)), ((), ())), preferred_element_type=jnp.float32
        ),
        "fsdp",
        scatter_dimension=0,
        tiled=True,
    )
    rows_dev = gradient.shape[0]
    moved = momentum_decay * momentum[0] + gradient
    coeffs = jnp.einsum(
        "rjn,kn->rjk", moved.reshape(rows_dev, blocks_row, SPAN), basis, precision=high
    )
    chosen = jnp.einsum("rjc,rjtc->rjt", coeffs, selector, precision=high)
    sent = jnp.einsum("rjt,rjtc->rjc", chosen, selector, precision=high)
    back = jnp.einsum("rjk,kn->rjn", sent, basis, precision=high).reshape(rows_dev, width)
    kept = moved - back
    values, places = (
        lax.all_gather(chosen[None], "rep", axis=0, tiled=True),
        lax.all_gather(picks[None], "rep", axis=0, tiled=True),
    )
    placed = (places[..., None] == slots).astype(jnp.float32)
    summed = jnp.einsum("arjt,arjtc->rjc", values, placed, precision=high)
    mean_sent = summed / lax.axis_size("rep")
    update = jnp.einsum("rjk,kn->rjn", mean_sent, basis, precision=high).reshape(rows_dev, width)
    return (params - learn_rate * update, kept[None])


def solution(mesh):
    in_specs = (
        P("rep", ("parts", "fsdp"), None),
        P("rep", ("parts", "fsdp"), None),
        P(("parts", "fsdp"), None),
        P("rep", ("parts", "fsdp"), None),
        P("rep", ("parts", "fsdp"), None, None),
    )
    out_specs = (P(("parts", "fsdp"), None), P("rep", ("parts", "fsdp"), None))
    return jax.shard_map(local, mesh=mesh, in_specs=in_specs, out_specs=out_specs, check_vma=False)
```

profile of v0, /device:TPU:0, one launch (start us, length us, event | category | flops | bytes accessed | tf_op | source)
XLA Modules:
  0.0 98.6 jit_solution(9816798639374426935)
XLA Ops:
  7.2 0.0 copy-start
  7.2 0.0 copy-start.4
  7.2 0.0 copy-start.1
  7.2 0.0 copy-start.2
  7.2 0.0 copy-start.3
  7.2 0.0 all-reduce.3.cloned.1.call-start
  7.3 1.7 %copy-done = bf16[1,256,5120]{2,1,0:T(8,128)(2,1)S(1)} copy-done((bf16[1,256,5120]{2,1,0:T(8,128)(2,1)S(1)}, bf16[1,256,5120]{2,1,0:T(8,128)(2,1)}, u32[]{:S(2)}) %copy-start) | copy-done | bytes 2621464
  8.9 1.8 %fusion = f32[8,5120]{1,0:T(8,128)} fusion(bf16[1,256,5120]{2,1,0:T(8,128)(2,1)S(1)} %copy-done, bf16[1,256,8]{1,2,0:T(8,128)(2,1)} %param.6), kind=kOutput, calls=%fused_computation | convolution fusion | flops 20971520 | bytes 2789376 | tf_op jit(solution)/shard_map/dot_general | solution.py:31
  10.7 0.0 all-reduce.3.cloned.1.call-update
  10.8 0.0 copy-done.1
  10.8 0.1 copy.9
  10.9 2.0 %all_gather.7 = s32[2,1,40,16]{2,3,1,0:T(8,128)S(1)} all-gather(s32[1,1,40,16]{2,3,1,0:T(8,128)S(1)} %copy-done.1), channel_id=1, replica_groups=mesh['parts'=2,'fsdp'=8,'rep'=2] {'rep'}, dimensions={0}, use_global_device_ids=true | all-gather | bytes 7680 | tf_op jit(solution)/shard_map/all_gather | solution.py:49
  12.8 0.1 copy.10
  12.9 0.0 copy-done.4
  12.9 0.6 dynamic-slice
  13.5 70.6 %all-reduce.3.cloned.1.call-done = f32[8,5120]{1,0:T(8,128)} async-done(((f32[8,5120]{1,0:T(8,128)}), f32[8,5120]{1,0:T(8,128)}) %all-reduce.3.cloned.1.call-update) | async-done | bytes 163856
  84.1 0.0 copy-done.2
  84.1 1.6 %dynamic-slice_add_fusion = f32[1,5120]{1,0:T(1,128)S(1)} fusion(f32[8,5120]{1,0:T(8,128)} %all-reduce.3.cloned.1.call-done, u32[]{:T(128)} %bitcast.19, f32[1,1,5120]{2,1,0:T(1,128)S(1)} %copy-done.2), kind=kLoop, calls=%fused_computation.23 | loop fusion | flops 10240 | bytes 61444 | tf_op jit(solution)/shard_map/add | solution.py:39
  85.7 0.5 fusion.9
  86.2 0.4 fusion.5
  86.7 0.1 copy.12
  86.7 0.1 copy.16
  86.8 0.4 fusion.4
  87.2 0.4 fusion.8
  87.6 0.6 subtract_bitcast_fusion
  88.3 1.8 %all-gather.1 = f32[2,40,16]{1,2,0:T(8,128)S(1)} all-gather(f32[1,40,16]{1,2,0:T(8,128)S(1)} %bitcast.35), channel_id=2, replica_groups=mesh['parts'=2,'fsdp'=8,'rep'=2] {'rep'}, dimensions={0}, use_global_device_ids=true | all-gather | bytes 7680 | tf_op jit(solution)/shard_map/all_gather | solution.py:48
  90.1 0.1 copy.13
  90.1 0.6 fusion.2
  90.7 0.4 convolution_multiply_fusion
  91.2 0.0 copy-done.3
  91.2 0.6 sub.6
  (1 shorter events, 0.0 us)
Async XLA Ops:
  7.2 1.8 %copy-start = (bf16[1,256,5120]{2,1,0:T(8,128)(2,1)S(1)}, bf16[1,256,5120]{2,1,0:T(8,128)(2,1)}, u32[]{:S(2)}) copy-start(bf16[1,256,5120]{2,1,0:T(8,128)(2,1)} %param.5) | copy-start | bytes 7864324
  7.2 5.7 %copy-start.4 = (u32[32]{0:T(128)S(1)}, u32[32]{0:T(128)}, u32[]{:S(2)}) copy-start(u32[32]{0:T(128)} %constant.28) | copy-start | bytes 388
  7.2 3.6 %copy-start.1 = (s32[1,1,40,16]{2,3,1,0:T(8,128)S(1)}, s32[1,1,40,16]{2,3,1,0:T(8,128)}, u32[]{:S(2)}) copy-start(s32[1,1,40,16]{2,3,1,0:T(8,128)} %param.9) | copy-start | bytes 7684
  7.2 76.9 %copy-start.2 = (f32[1,1,5120]{2,1,0:T(1,128)S(1)}, f32[1,1,5120]{2,1,0:T(1,128)}, u32[]{:S(2)}) copy-start(f32[1,1,5120]{2,1,0:T(1,128)} %param.8) | copy-start | bytes 61444
  7.2 84.0 %copy-start.3 = (f32[1,5120]{1,0:T(1,128)S(1)}, f32[1,5120]{1,0:T(1,128)}, u32[]{:S(2)}) copy-start(f32[1,5120]{1,0:T(1,128)} %param.7) | copy-start | bytes 61444
  7.2 76.9 %all-reduce.3.cloned.1.call-start = ((), (), s32[]{:S(2)}) async-start(), calls=%async_computation | async-start | bytes 327680
Sparse Core Ops, SparseCore 0:
  11.4 72.7 all-reduce.2
where the time goes:
time: 98.9 us; the launch traced here: 98.6 us
  waiting for transfers between devices  70.7 us (71%)
  between operations  14.1 us (14%)
  matrix products  4.54 us (5%)
  blocking collectives  3.76 us (4%)
  other arithmetic  2.87 us (3%)
  local copies, waits for them, and re-layouts  2.65 us (3%)
    unnamed x2, waiting for transfers between devices  70.7 us
    unnamed x11, local copies, waits for them, and re-layouts  2.27 us
  transfers between devices with their start and end apart: 1, of which 1 were waited for; matrix products, arithmetic and copies ran while one was open for 1% of the time, Pallas kernels for 0%

commit v1 on v0

v1 whole, which is shorter than its diff:
```python
import functools

import jax
import jax.numpy as jnp
import numpy as np
from jax import lax
from jax.experimental import pallas as pl
from jax.experimental.pallas import tpu as pltpu
from jax.sharding import PartitionSpec as P

MESH = pl.DeviceIdType.MESH

momentum_decay = 0.9
learn_rate = 0.5


def split_basis(length):
    freq = np.arange(length, dtype=np.float64)[:, None]
    place = np.arange(length, dtype=np.float64)[None, :]
    scale = np.where(freq == 0.0, np.sqrt(1.0 / length), np.sqrt(2.0 / length))
    basis = scale * np.cos(np.pi * (2.0 * place + 1.0) * freq / (2.0 * length))

    def stacked(b):
        high = b.astype(jnp.bfloat16)
        low = (b - high.astype(np.float64)).astype(jnp.bfloat16)
        both = np.concatenate([high, low], axis=1)
        return np.concatenate([both, both], axis=0)

    return stacked(basis.T), stacked(basis)


def times(x, w, span):
    high = x.astype(jnp.bfloat16)
    low = (x - high.astype(jnp.float32)).astype(jnp.bfloat16)
    out = jnp.dot(
        jnp.concatenate([high, low], axis=1), w, preferred_element_type=jnp.float32
    )
    return out[:, :span] + out[:, span:]


def kernel(
    n, reps, tok_hbm, cot_hbm, par_hbm, mom_hbm, idx_hbm, wf_hbm, wb_hbm,
    newp_hbm, newm_hbm,
    tok, cot, par, mom, idx, wf, wb, newp, newm, send, recv, back, peer, mask,
    tok_sem, in_sem, out_sem, send_sem, recv_sem, bsend_sem, brecv_sem,
):
    me = lax.axis_index("fsdp")
    my_rep = lax.axis_index("rep")
    chunks, _, rows_dev, cb, span = send.shape
    rows = n * rows_dev
    cols = cb * span

    barrier = pltpu.get_barrier_semaphore()

    def greet(d):
        pl.semaphore_signal(
            barrier, inc=1, device_id={"fsdp": lax.rem(me + d, n)}, device_id_type=MESH
        )

    def over_peers(body):
        if n <= 16:
            for d in range(n - 1, 0, -1):
                body(d)
        else:
            lax.fori_loop(1, n, lambda d, c: (body(d), c)[1], 0)

    small = [(cot_hbm, cot), (par_hbm, par), (mom_hbm, mom), (idx_hbm, idx), (wf_hbm, wf), (wb_hbm, wb)]
    in_copies = [
        pltpu.make_async_copy(src, dst, in_sem.at[i]) for i, (src, dst) in enumerate(small)
    ]
    tok_copies = [
        pltpu.make_async_copy(
            tok_hbm.at[:, pl.ds(c * cols, cols)], tok.at[c], tok_sem.at[c]
        )
        for c in range(chunks)
    ]
    over_peers(greet)
    for a in range(1, reps):
        pl.semaphore_signal(
            barrier, inc=1, device_id={"rep": lax.rem(my_rep + a, reps)}, device_id_type=MESH
        )
    in_copies[0].start()
    for c in range(chunks):
        tok_copies[c].start()
    for i in range(1, len(small)):
        in_copies[i].start()

    in_copies[0].wait()
    lhs = cot[...]
    for c in range(chunks):
        tok_copies[c].wait()
        part = jnp.dot(lhs, tok[c], preferred_element_type=jnp.float32)
        for j in range(cb):
            send[c, :, :, j, :] = part[:, j * span : (j + 1) * span].reshape(n, rows_dev, span)
        if c == 0:
            pl.semaphore_wait(barrier, n - 1 + reps - 1)

        def scatter(d, c=c):
            to = lax.rem(me + d, n)
            pltpu.make_async_remote_copy(
                src_ref=send.at[c, to],
                dst_ref=recv.at[c, d - 1],
                send_sem=send_sem.at[c],
                recv_sem=recv_sem.at[c],
                device_id={"fsdp": to},
                device_id_type=MESH,
            ).start()

        over_peers(scatter)

    for i in range(1, len(small)):
        in_copies[i].wait()
    slots = lax.broadcasted_iota(jnp.int32, (cb, span), 1)
    for r in range(rows_dev):
        turned = idx[r].T
        for c in range(chunks):
            picks = turned[c * cb : (c + 1) * cb, :]
            hit = picks[:, 0:1] == slots
            for t in range(1, picks.shape[1]):
                hit = jnp.logical_or(hit, picks[:, t : t + 1] == slots)
            mask[c, r * cb : (r + 1) * cb, :] = hit.astype(jnp.float32)

    def scattered(c):
        return pltpu.make_async_remote_copy(
            src_ref=send.at[c, pl.ds(0, n - 1)],
            dst_ref=recv.at[c, pl.ds(0, n - 1)],
            send_sem=send_sem.at[c],
            recv_sem=recv_sem.at[c],
            device_id={"fsdp": lax.rem(me + 1, n)},
            device_id_type=MESH,
        )

    def swap(c, a):
        return pltpu.make_async_remote_copy(
            src_ref=back.at[c],
            dst_ref=peer.at[a - 1, c],
            send_sem=bsend_sem.at[a - 1, c],
            recv_sem=brecv_sem.at[a - 1, c],
            device_id={"rep": lax.rem(my_rep + a, reps)},
            device_id_type=MESH,
        )

    for c in range(chunks):
        blocks = pl.ds(c * cb, cb)
        mine = send[c, me] + momentum_decay * mom[:, blocks, :]
        scattered(c).wait_recv()
        moved = mine + jnp.sum(recv[c], axis=0)
        moved = moved.reshape(rows_dev * cb, span)
        coeffs = times(moved, wf[...], span)
        sent = coeffs * mask[c]
        undone = times(sent, wb[...], span)
        back[c] = undone
        for a in range(1, reps):
            swap(c, a).start()
        newm[:, blocks, :] = (moved - undone).reshape(rows_dev, cb, span)
    newm_copy = pltpu.make_async_copy(newm, newm_hbm, out_sem.at[0])
    newm_copy.start()
    for c in range(chunks):
        blocks = pl.ds(c * cb, cb)
        total = back[c]
        for a in range(1, reps):
            swap(c, a).wait_recv()
            total = total + peer[a - 1, c]
        newp[:, blocks, :] = par[:, blocks, :] - (learn_rate / reps) * total.reshape(
            rows_dev, cb, span
        )
    newp_copy = pltpu.make_async_copy(newp, newp_hbm, out_sem.at[1])
    newp_copy.start()
    for c in range(chunks):
        scattered(c).wait_send()
        for a in range(1, reps):
            swap(c, a).wait_send()
    newm_copy.wait()
    newp_copy.wait()


def local(n, reps, tokens, cotangent, params, momentum, indices):
    _, count, width = tokens.shape
    rows_dev, blocks_row, topk = indices.shape[1:]
    span = width // blocks_row
    cb = 8 if blocks_row % 8 == 0 else blocks_row
    chunks = blocks_row // cb
    rows = cotangent.shape[2]
    wf, wb = split_basis(span)
    shape = (rows_dev, blocks_row, span)
    f32 = jnp.float32
    anywhere = pl.BlockSpec(memory_space=pl.ANY)
    newp, newm = pl.pallas_call(
        functools.partial(kernel, n, reps),
        out_shape=[jax.ShapeDtypeStruct(shape, f32)] * 2,
        in_specs=[anywhere] * 7,
        out_specs=[anywhere] * 2,
        scratch_shapes=[
            pltpu.VMEM((chunks, count, cb * span), tokens.dtype),
            pltpu.VMEM((rows, count), cotangent.dtype),
            pltpu.VMEM(shape, f32),
            pltpu.VMEM(shape, f32),
            pltpu.VMEM((rows_dev, topk, blocks_row), indices.dtype),
            pltpu.VMEM(wf.shape, jnp.bfloat16),
            pltpu.VMEM(wb.shape, jnp.bfloat16),
            pltpu.VMEM(shape, f32),
            pltpu.VMEM(shape, f32),
            pltpu.VMEM((chunks, n, rows_dev, cb, span), f32),
            pltpu.VMEM((chunks, n - 1, rows_dev, cb, span), f32),
            pltpu.VMEM((chunks, rows_dev * cb, span), f32),
            pltpu.VMEM((reps - 1, chunks, rows_dev * cb, span), f32),
            pltpu.VMEM((chunks, rows_dev * cb, span), f32),
            pltpu.SemaphoreType.DMA((chunks,)),
            pltpu.SemaphoreType.DMA((6,)),
            pltpu.SemaphoreType.DMA((2,)),
            pltpu.SemaphoreType.DMA((chunks,)),
            pltpu.SemaphoreType.DMA((chunks,)),
            pltpu.SemaphoreType.DMA((reps - 1, chunks)),
            pltpu.SemaphoreType.DMA((reps - 1, chunks)),
        ],
        compiler_params=pltpu.CompilerParams(collective_id=0, has_side_effects=True),
    )(
        tokens[0],
        cotangent[0].T,
        params.reshape(shape),
        momentum.reshape(shape),
        indices[0].transpose(0, 2, 1),
        jnp.asarray(wf),
        jnp.asarray(wb),
    )
    return newp.reshape(rows_dev, width), newm.reshape(1, rows_dev, width)


def solution(mesh):
    in_specs = (
        P("rep", ("parts", "fsdp"), None),
        P("rep", ("parts", "fsdp"), None),
        P(("parts", "fsdp"), None),
        P("rep", ("parts", "fsdp"), None),
        P("rep", ("parts", "fsdp"), None, None),
    )
    out_specs = (P(("parts", "fsdp"), None), P("rep", ("parts", "fsdp"), None))
    body = functools.partial(local, mesh.shape["fsdp"], mesh.shape["rep"])
    return jax.shard_map(body, mesh=mesh, in_specs=in_specs, out_specs=out_specs, check_vma=False)
```

time: 98.9 us -> 16.2 us (0.16)
  the two profiles are of different devices: /device:TPU:0 before, /device:TPU:1 now
where the time goes in v1:
time: 16.2 us; the launch traced here: 15.9 us
  Pallas kernels  12.6 us (78%)
  local copies, waits for them, and re-layouts  2.67 us (16%)
  between operations  0.64 us (4%)
    pallas_call x1, Pallas kernels, local(): pl.pallas_call(functools.partial(kernel, n, reps), out_shape=[jax.ShapeDt...  12.6 us
    unnamed x2, local copies, waits for them, and re-layouts  2.67 us

profile of v1, /device:TPU:1, one launch (start us, length us, event | category | flops | bytes accessed | tf_op | source)
XLA Modules:
  0.0 15.9 jit_solution(7248550848729927991)
XLA Ops:
  0.6 12.6 %shard_map.86 = (f32[1,40,128]{2,1,0:T(8,128)}, f32[1,40,128]{2,1,0:T(8,128)}) custom-call(bf16[256,5120]{1,0:T(8,128)(2,1)} %bitcast.11, bf16[8,256]{1,0:T(8,128)(2,1)} %bitcast.17, f32[1,40,128]{2,1,0:T(8,128)} %bitcast.12, f32[1,40,128]{2,1,0:T(8,128)} %bitcast.13, s32[1,16,40]{2,1,0:T(8,128)} %bitcast.16, bf16[256,256]{1,0:T(8,128)(2,1)} %constant.4.clone.wf_hbm, ...), custom_call_target="tpu_custom_call" | custom-call | tf_op jit(solution)/shard_map/pallas_call | solution.py:188
  13.3 1.3 %copy.11 = f32[1,5120]{1,0:T(1,128)} copy(f32[1,5120]{1,0:T(1,128)} %bitcast.15) | data formatting | bytes 40960
  14.6 1.3 %copy.12 = f32[1,1,5120]{2,1,0:T(1,128)} copy(f32[1,1,5120]{2,1,0:T(1,128)} %bitcast.14) | data formatting | bytes 40960

commit v2 on v1

--- a/solution.py
+++ b/solution.py
@@ -40,9 +40,9 @@
 
 def kernel(
     n, reps, tok_hbm, cot_hbm, par_hbm, mom_hbm, idx_hbm, wf_hbm, wb_hbm,
-    newp_hbm, newm_hbm,
-    tok, cot, par, mom, idx, wf, wb, newp, newm, send, recv, back, peer, mask,
-    tok_sem, in_sem, out_sem, send_sem, recv_sem, bsend_sem, brecv_sem,
+    newp, newm,
+    tok, cot, par, mom, idx, wf, wb, send, recv, back, peer, mask,
+    tok_sem, in_sem, send_sem, recv_sem, bsend_sem, brecv_sem,
 ):
     me = lax.axis_index("fsdp")
     my_rep = lax.axis_index("rep")
@@ -153,8 +153,6 @@
         for a in range(1, reps):
             swap(c, a).start()
         newm[:, blocks, :] = (moved - undone).reshape(rows_dev, cb, span)
-    newm_copy = pltpu.make_async_copy(newm, newm_hbm, out_sem.at[0])
-    newm_copy.start()
     for c in range(chunks):
         blocks = pl.ds(c * cb, cb)
         total = back[c]
@@ -164,14 +162,21 @@
         newp[:, blocks, :] = par[:, blocks, :] - (learn_rate / reps) * total.reshape(
             rows_dev, cb, span
         )
-    newp_copy = pltpu.make_async_copy(newp, newp_hbm, out_sem.at[1])
-    newp_copy.start()
     for c in range(chunks):
         scattered(c).wait_send()
         for a in range(1, reps):
             swap(c, a).wait_send()
-    newm_copy.wait()
-    newp_copy.wait()
+
+
+def put(newp, newm, newp_hbm, newm_hbm, out_sem):
+    copies = [
+        pltpu.make_async_copy(newp, newp_hbm, out_sem.at[0]),
+        pltpu.make_async_copy(newm, newm_hbm, out_sem.at[1]),
+    ]
+    for copy in copies:
+        copy.start()
+    for copy in copies:
+        copy.wait()
 
 
 def local(n, reps, tokens, cotangent, params, momentum, indices):
@@ -184,12 +189,22 @@
     wf, wb = split_basis(span)
     shape = (rows_dev, blocks_row, span)
     f32 = jnp.float32
-    anywhere = pl.BlockSpec(memory_space=pl.ANY)
+    remote = pl.BlockSpec(memory_space=pltpu.HBM)
+    near = pl.BlockSpec(memory_space=pltpu.VMEM)
+    operands = (
+        tokens[0],
+        cotangent[0].T,
+        params.reshape(shape),
+        momentum.reshape(shape),
+        indices[0].transpose(0, 2, 1),
+        jnp.asarray(wf),
+        jnp.asarray(wb),
+    )
     newp, newm = pl.pallas_call(
         functools.partial(kernel, n, reps),
         out_shape=[jax.ShapeDtypeStruct(shape, f32)] * 2,
-        in_specs=[anywhere] * 7,
-        out_specs=[anywhere] * 2,
+        in_specs=[remote] * len(operands),
+        out_specs=[near] * 2,
         scratch_shapes=[
             pltpu.VMEM((chunks, count, cb * span), tokens.dtype),
             pltpu.VMEM((rows, count), cotangent.dtype),
@@ -198,8 +213,6 @@
             pltpu.VMEM((rows_dev, topk, blocks_row), indices.dtype),
             pltpu.VMEM(wf.shape, jnp.bfloat16),
             pltpu.VMEM(wb.shape, jnp.bfloat16),
-            pltpu.VMEM(shape, f32),
-            pltpu.VMEM(shape, f32),
             pltpu.VMEM((chunks, n, rows_dev, cb, span), f32),
             pltpu.VMEM((chunks, n - 1, rows_dev, cb, span), f32),
             pltpu.VMEM((chunks, rows_dev * cb, span), f32),
@@ -207,22 +220,23 @@
             pltpu.VMEM((chunks, rows_dev * cb, span), f32),
             pltpu.SemaphoreType.DMA((chunks,)),
             pltpu.SemaphoreType.DMA((6,)),
-            pltpu.SemaphoreType.DMA((2,)),
             pltpu.SemaphoreType.DMA((chunks,)),
             pltpu.SemaphoreType.DMA((chunks,)),
             pltpu.SemaphoreType.DMA((reps - 1, chunks)),
             pltpu.SemaphoreType.DMA((reps - 1, chunks)),
         ],
-        compiler_params=pltpu.CompilerParams(collective_id=0, has_side_effects=True),
-    )(
-        tokens[0],
-        cotangent[0].T,
-        params.reshape(shape),
-        momentum.reshape(shape),
-        indices[0].transpose(0, 2, 1),
-        jnp.asarray(wf),
-        jnp.asarray(wb),
-    )
+        compiler_params=pltpu.CompilerParams(
+            collective_id=0, has_side_effects=True, vmem_limit_bytes=24 << 20
+        ),
+    )(*(pltpu.with_memory_space_constraint(x, pltpu.HBM) for x in operands))
+    newp, newm = pl.pallas_call(
+        put,
+        out_shape=[jax.ShapeDtypeStruct(shape, f32)] * 2,
+        in_specs=[near] * 2,
+        out_specs=[remote] * 2,
+        scratch_shapes=[pltpu.SemaphoreType.DMA((2,))],
+        compiler_params=pltpu.CompilerParams(vmem_limit_bytes=1 << 20),
+    )(newp, newm)
     return newp.reshape(rows_dev, width), newm.reshape(1, rows_dev, width)
 
 

time: 16.2 us -> 13.6 us (0.84)
  the two profiles are of different devices: /device:TPU:1 before, /device:TPU:0 now
where the time goes in v2:
time: 13.6 us; the launch traced here: 13.4 us
  Pallas kernels  12.8 us (94%)
  between operations  0.64 us (5%)
    pallas_call x1, Pallas kernels, local(): pl.pallas_call(functools.partial(kernel, n, reps), out_shape=[jax.ShapeDt...  12.2 us
    pallas_call x1, Pallas kernels, local(): pl.pallas_call(put, out_shape=[jax.ShapeDtypeStruct(shape, f32)] * 2, in_...  0.63 us

profile of v2, /device:TPU:0, one launch (start us, length us, event | category | flops | bytes accessed | tf_op | source)
XLA Modules:
  0.0 13.4 jit_solution(12605480603314879486)
XLA Ops:
  0.6 12.2 %shard_map.86 = (f32[1,40,128]{2,1,0:T(8,128)S(1)}, f32[1,40,128]{2,1,0:T(8,128)S(1)}) custom-call(bf16[256,5120]{1,0:T(8,128)(2,1)} %bitcast.11, bf16[8,256]{1,0:T(8,128)(2,1)} %bitcast.15, f32[1,40,128]{2,1,0:T(8,128)} %bitcast.12, f32[1,40,128]{2,1,0:T(8,128)} %bitcast.13, s32[1,16,40]{2,1,0:T(8,128)} %bitcast.14, bf16[256,256]{1,0:T(8,128)(2,1)} %constant.4.clone.wf_hbm, ...), custom_call_target="tpu_custom_call" | custom-call | tf_op jit(solution)/shard_map/pallas_call | solution.py:203
  12.8 0.6 %shard_map.87 = (f32[1,40,128]{2,1,0:T(8,128)}, f32[1,40,128]{2,1,0:T(8,128)}) custom-call(f32[1,40,128]{2,1,0:T(8,128)S(1)} %get-tuple-element.6.newp, f32[1,40,128]{2,1,0:T(8,128)S(1)} %get-tuple-element.7.newm), custom_call_target="tpu_custom_call" | custom-call | tf_op jit(solution)/shard_map/pallas_call | solution.py:232

commit v3 on v2

--- a/solution.py
+++ b/solution.py
@@ -57,12 +57,12 @@
             barrier, inc=1, device_id={"fsdp": lax.rem(me + d, n)}, device_id_type=MESH
         )
 
-    def over_peers(body):
+    def over_peers(body, first=1, last=n):
         if n <= 16:
-            for d in range(n - 1, 0, -1):
+            for d in range(first, last):
                 body(d)
         else:
-            lax.fori_loop(1, n, lambda d, c: (body(d), c)[1], 0)
+            lax.fori_loop(first, last, lambda d, c: (body(d), c)[1], 0)
 
     small = [(cot_hbm, cot), (par_hbm, par), (mom_hbm, mom), (idx_hbm, idx), (wf_hbm, wf), (wb_hbm, wb)]
     in_copies = [
@@ -85,6 +85,19 @@
     for i in range(1, len(small)):
         in_copies[i].start()
 
+    def scatter(d, c):
+        past = (d - 1 + n - me) // n
+        to = d - 1 + past
+        pltpu.make_async_remote_copy(
+            src_ref=send.at[c, to],
+            dst_ref=recv.at[c, me - 1 + past],
+            send_sem=send_sem.at[c],
+            recv_sem=recv_sem.at[c],
+            device_id={"fsdp": to},
+            device_id_type=MESH,
+        ).start()
+
+    early = min(1, n - 1)
     in_copies[0].wait()
     lhs = cot[...]
     for c in range(chunks):
@@ -95,18 +108,9 @@
         if c == 0:
             pl.semaphore_wait(barrier, n - 1 + reps - 1)
 
-        def scatter(d, c=c):
-            to = lax.rem(me + d, n)
-            pltpu.make_async_remote_copy(
-                src_ref=send.at[c, to],
-                dst_ref=recv.at[c, d - 1],
-                send_sem=send_sem.at[c],
-                recv_sem=recv_sem.at[c],
-                device_id={"fsdp": to},
-                device_id_type=MESH,
-            ).start()
-
-        over_peers(scatter)
+        over_peers(functools.partial(scatter, c=c), 1, 1 + early)
+    for c in range(chunks):
+        over_peers(functools.partial(scatter, c=c), 1 + early, n)
 
     for i in range(1, len(small)):
         in_copies[i].wait()
@@ -118,7 +122,7 @@
             hit = picks[:, 0:1] == slots
             for t in range(1, picks.shape[1]):
                 hit = jnp.logical_or(hit, picks[:, t : t + 1] == slots)
-            mask[c, r * cb : (r + 1) * cb, :] = hit.astype(jnp.float32)
+            mask[(c * rows_dev + r) * cb : (c * rows_dev + r + 1) * cb, :] = hit.astype(jnp.float32)
 
     def scattered(c):
         return pltpu.make_async_remote_copy(
@@ -130,42 +134,42 @@
             device_id_type=MESH,
         )
 
-    def swap(c, a):
+    def swap(a):
         return pltpu.make_async_remote_copy(
-            src_ref=back.at[c],
-            dst_ref=peer.at[a - 1, c],
-            send_sem=bsend_sem.at[a - 1, c],
-            recv_sem=brecv_sem.at[a - 1, c],
+            src_ref=back,
+            dst_ref=peer.at[a - 1],
+            send_sem=bsend_sem.at[a - 1],
+            recv_sem=brecv_sem.at[a - 1],
             device_id={"rep": lax.rem(my_rep + a, reps)},
             device_id_type=MESH,
         )
 
+    parts = []
+    for c in range(chunks):
+        mine = send[c, me] + momentum_decay * mom[:, pl.ds(c * cb, cb), :]
+        scattered(c).wait_recv()
+        parts.append((mine + jnp.sum(recv[c], axis=0)).reshape(rows_dev * cb, span))
+    moved = jnp.concatenate(parts, axis=0)
+    sent = times(moved, wf[...], span) * mask[...]
+    undone = times(sent, wb[...], span)
+    back[...] = undone
+    for a in range(1, reps):
+        swap(a).start()
+    kept = moved - undone
+    size = rows_dev * cb
+    for c in range(chunks):
+        newm[:, pl.ds(c * cb, cb), :] = kept[c * size : (c + 1) * size].reshape(rows_dev, cb, span)
+        scattered(c).wait_send()
+    for a in range(1, reps):
+        swap(a).wait_recv()
+        undone = undone + peer[a - 1]
     for c in range(chunks):
         blocks = pl.ds(c * cb, cb)
-        mine = send[c, me] + momentum_decay * mom[:, blocks, :]
-        scattered(c).wait_recv()
-        moved = mine + jnp.sum(recv[c], axis=0)
-        moved = moved.reshape(rows_dev * cb, span)
-        coeffs = times(moved, wf[...], span)
-        sent = coeffs * mask[c]
-        undone = times(sent, wb[...], span)
-        back[c] = undone
-        for a in range(1, reps):
-            swap(c, a).start()
-        newm[:, blocks, :] = (moved - undone).reshape(rows_dev, cb, span)
-    for c in range(chunks):
-        blocks = pl.ds(c * cb, cb)
-        total = back[c]
-        for a in range(1, reps):
-            swap(c, a).wait_recv()
-            total = total + peer[a - 1, c]
-        newp[:, blocks, :] = par[:, blocks, :] - (learn_rate / reps) * total.reshape(
-            rows_dev, cb, span
-        )
-    for c in range(chunks):
-        scattered(c).wait_send()
-        for a in range(1, reps):
-            swap(c, a).wait_send()
+        newp[:, blocks, :] = par[:, blocks, :] - (learn_rate / reps) * undone[
+            c * size : (c + 1) * size
+        ].reshape(rows_dev, cb, span)
+    for a in range(1, reps):
+        swap(a).wait_send()
 
 
 def put(newp, newm, newp_hbm, newm_hbm, out_sem):
@@ -215,15 +219,15 @@
             pltpu.VMEM(wb.shape, jnp.bfloat16),
             pltpu.VMEM((chunks, n, rows_dev, cb, span), f32),
             pltpu.VMEM((chunks, n - 1, rows_dev, cb, span), f32),
-            pltpu.VMEM((chunks, rows_dev * cb, span), f32),
-            pltpu.VMEM((reps - 1, chunks, rows_dev * cb, span), f32),
-            pltpu.VMEM((chunks, rows_dev * cb, span), f32),
+            pltpu.VMEM((rows_dev * blocks_row, span), f32),
+            pltpu.VMEM((reps - 1, rows_dev * blocks_row, span), f32),
+            pltpu.VMEM((rows_dev * blocks_row, span), f32),
             pltpu.SemaphoreType.DMA((chunks,)),
             pltpu.SemaphoreType.DMA((6,)),
             pltpu.SemaphoreType.DMA((chunks,)),
             pltpu.SemaphoreType.DMA((chunks,)),
-            pltpu.SemaphoreType.DMA((reps - 1, chunks)),
-            pltpu.SemaphoreType.DMA((reps - 1, chunks)),
+            pltpu.SemaphoreType.DMA((reps - 1,)),
+            pltpu.SemaphoreType.DMA((reps - 1,)),
         ],
         compiler_params=pltpu.CompilerParams(
             collective_id=0, has_side_effects=True, vmem_limit_bytes=24 << 20

time: 13.6 us -> 12.7 us (0.934)
  the two profiles are of different devices: /device:TPU:0 before, /device:TPU:3 now
where the time goes in v3:
time: 12.7 us; the launch traced here: 12.5 us
  Pallas kernels  11.9 us (94%)
  between operations  0.64 us (5%)
    pallas_call x1, Pallas kernels, local(): pl.pallas_call(functools.partial(kernel, n, reps), out_shape=[jax.ShapeDt...  11.2 us
    pallas_call x1, Pallas kernels, local(): pl.pallas_call(put, out_shape=[jax.ShapeDtypeStruct(shape, f32)] * 2, in_...  0.63 us

profile of v3, /device:TPU:3, one launch (start us, length us, event | category | flops | bytes accessed | tf_op | source)
XLA Modules:
  0.0 12.5 jit_solution(12216914503915996289)
XLA Ops:
  0.6 11.2 %shard_map.86 = (f32[1,40,128]{2,1,0:T(8,128)S(1)}, f32[1,40,128]{2,1,0:T(8,128)S(1)}) custom-call(bf16[256,5120]{1,0:T(8,128)(2,1)} %bitcast.11, bf16[8,256]{1,0:T(8,128)(2,1)} %bitcast.15, f32[1,40,128]{2,1,0:T(8,128)} %bitcast.12, f32[1,40,128]{2,1,0:T(8,128)} %bitcast.13, s32[1,16,40]{2,1,0:T(8,128)} %bitcast.14, bf16[256,256]{1,0:T(8,128)(2,1)} %constant.4.clone.wf_hbm, ...), custom_call_target="tpu_custom_call" | custom-call | tf_op jit(solution)/shard_map/pallas_call | solution.py:207
  11.9 0.6 %shard_map.87 = (f32[1,40,128]{2,1,0:T(8,128)}, f32[1,40,128]{2,1,0:T(8,128)}) custom-call(f32[1,40,128]{2,1,0:T(8,128)S(1)} %get-tuple-element.6.newp, f32[1,40,128]{2,1,0:T(8,128)S(1)} %get-tuple-element.7.newm), custom_call_target="tpu_custom_call" | custom-call | tf_op jit(solution)/shard_map/pallas_call | solution.py:236
